TPU v7x, 32 devices: a whole 2x2x4 slice. The times are simulated.
32 devices in a mesh: gx: 8 (over z, x), gy: 4 (over y, core).
Axes of the slice: x: 2, y: 2, z: 4, core: 2. Of those that a mesh axis runs over, the one named last changes fastest.
Arguments:
- pooled: bfloat16 [4096, 8, 128], P(('gx', 'gy')), may hold values from -6 to 6
- cotangent: bfloat16 [4096, 28, 128], P(('gx', 'gy')), may hold values from -0.09375 to 0.09375
- bilinear: bfloat16 [7, 128, 128], replicated, may hold values from -0.5 to 0.5
- bag_ids: int32 [4096, 8, 4], P(('gx', 'gy')), may hold values from 0 to 8191, as said below
- bag_lens: int32 [4096, 8], P(('gx', 'gy')), may hold values from 1 to 4
- row_home: int32 [8, 8192], replicated, may hold values from 0 to 8191, as said below
Outputs:
- weight_grad: float32 [7, 128, 128], replicated
- table_grad: float32 [8192, 8, 128], P(('gx', 'gy'))
Inputs may be any that keep to these rules, and one draw needn't show every extreme that they name: Each row row_home[f] is a permutation; row r of field f's table is stored at position row_home[f, r] of table_grad's first dimension. Only the first bag_lens entries of a bag are live. The stored position q = row_home[f, bag_ids[sample, f, k]] of an entry lies in the block of 256 positions of device q // 256 (devices in gx+gy order); among all entries of one device's samples, live or not, at most 256 lie in any one device's block; in every device's entries some block is hit exactly 256 times, and one block is hit exactly 256 times by the entries of every device.
All inputs are finite; a program needn't handle non-finite values.
Results may differ from a plain program's by a relative error of at most 0.0035.
Values may be sent and summed in bfloat16 or wider, within the bound.
No kernel may reach another device: no remote copies, remote signals or barrier semaphores. Data moves between devices by JAX's collectives and lax.ppermute only.
A program may use at most 64 MiB of HBM per device.

v0:
```python
import jax
import jax.numpy as jnp
from jax import lax
from jax.sharding import PartitionSpec as P

FIELDS = 8
BAG = 4
R_DEV = 256


def pair_list(fields):
    return [(i, j) for i in range(fields) for j in range(i + 1, fields)]


def on_device(pooled, cotangent, bilinear, bag_ids, bag_lens, row_home):
    pair_order = pair_list(FIELDS)
    samples = pooled.shape[0]
    width = pooled.shape[2]
    projected = jnp.einsum(
        "bfd,fde->bfe", pooled[:, : FIELDS - 1], bilinear, preferred_element_type=jnp.float32
    )
    upper_terms = []
    for i in range(FIELDS - 1):
        running = jnp.zeros((samples, width), jnp.float32)
        for p, (a, c) in enumerate(pair_order):
            if a == i:
                running = running + cotangent[:, p].astype(jnp.float32) * pooled[:, c].astype(
                    jnp.float32
                )
        upper_terms.append(running)
    upper_bf = jnp.stack(upper_terms, 1).astype(jnp.bfloat16)
    local_weight = jnp.einsum(
        "bfd,bfe->fde", pooled[:, : FIELDS - 1], upper_bf, preferred_element_type=jnp.float32
    )
    weight_grad = lax.psum(local_weight, ("gx", "gy"))
    back_terms = jnp.einsum("bfe,fde->bfd", upper_bf, bilinear, preferred_element_type=jnp.float32)
    field_list = []
    for i in range(FIELDS):
        running = back_terms[:, i] if i < FIELDS - 1 else jnp.zeros((samples, width), jnp.float32)
        for p, (a, c) in enumerate(pair_order):
            if c == i:
                running = running + cotangent[:, p].astype(jnp.float32) * projected[:, a]
        field_list.append(running)
    field_grads = jnp.stack(field_list, 1).astype(jnp.bfloat16)
    size_gx = lax.axis_size("gx")
    size_gy = lax.axis_size("gy")
    owners_all = size_gx * size_gy
    entries = samples * FIELDS * BAG
    capacity = max(1, 2 * entries // owners_all)
    sentinel = R_DEV * FIELDS
    field_index = jnp.arange(FIELDS, dtype=jnp.int32)[None, :, None]
    stored = row_home[field_index, bag_ids]
    live = jnp.arange(BAG, dtype=jnp.int32)[None, None, :] < bag_lens[:, :, None]
    owner = (stored // R_DEV).reshape(-1)
    target = jnp.where(live, stored % R_DEV * FIELDS + field_index, sentinel).reshape(-1)
    values = jnp.where(live[:, :, :, None], field_grads[:, :, None, :], jnp.zeros((), jnp.bfloat16))
    values = values.reshape(entries, width)
    block_rows = 128
    blocks = entries // block_rows
    owner_ids = jnp.arange(owners_all, dtype=jnp.int32)
    owner_table = (owner.reshape(blocks, block_rows, 1) == owner_ids[None, None, :]).astype(
        jnp.bfloat16
    )
    row_pos = jnp.arange(block_rows, dtype=jnp.int32)
    earlier = (row_pos[:, None] > row_pos[None, :]).astype(jnp.bfloat16)
    within_all = jnp.einsum("ij,bjo->bio", earlier, owner_table, preferred_element_type=jnp.float32)
    block_totals = jnp.sum(owner_table.astype(jnp.float32), axis=1)
    block_start = jnp.cumsum(block_totals, axis=0) - block_totals
    ahead = within_all + block_start[:, None, :]
    rank = jnp.sum(ahead * owner_table.astype(jnp.float32), axis=2).reshape(-1).astype(jnp.int32)
    place = owner * capacity + rank
    send_values = (
        jnp.zeros((owners_all * capacity, width), jnp.bfloat16)
        .at[place]
        .set(values, unique_indices=True)
    )
    send_target = (
        jnp.full((owners_all * capacity,), sentinel, jnp.int32)
        .at[place]
        .set(target, unique_indices=True)
    )
    send_values = send_values.reshape(size_gx, size_gy, capacity, width)
    send_target = send_target.reshape(size_gx, size_gy, capacity)
    got_values, got_target = (
        lax.all_to_all(
            lax.all_to_all(send_values, "gy", split_axis=1, concat_axis=1, tiled=True),
            "gx",
            split_axis=0,
            concat_axis=0,
            tiled=True,
        ),
        lax.all_to_all(
            lax.all_to_all(send_target, "gy", split_axis=1, concat_axis=1, tiled=True),
            "gx",
            split_axis=0,
            concat_axis=0,
            tiled=True,
        ),
    )
    summed = jax.ops.segment_sum(
        got_values.reshape(-1, width).astype(jnp.float32),
        got_target.reshape(-1),
        num_segments=sentinel + 1,
    )
    table_grad = summed[:sentinel].reshape(R_DEV, FIELDS, width)
    return (weight_grad, table_grad)


def solution(mesh):
    placed = (
        P(("gx", "gy"), None, None),
        P(("gx", "gy"), None, None),
        P(),
        P(("gx", "gy"), None, None),
        P(("gx", "gy"), None),
        P(),
    )
    return jax.shard_map(
        on_device,
        mesh=mesh,
        in_specs=placed,
        out_specs=(P(), P(("gx", "gy"), None, None)),
        check_vma=False,
    )
```

profile of v0, /device:TPU:0, one launch (start us, length us, event | category | flops | bytes accessed | tf_op | source)
XLA Modules:
  0.0 339.2 jit_solution(13678758075913814048)
XLA Ops:
  7.2 0.8 fusion.102
  8.5 25.5 %gather_fusion = s32[4096]{0:T(1024)S(1)} fusion(s32[8,8192]{1,0:T(8,128)S(1)} %copy-done, s32[4096]{0:T(1024)S(1)} %reshape.231), kind=kCustom, calls=%fused_computation | custom fusion | bytes 65536 | tf_op jit(solution)/shard_map/gather | solution.py:52
  34.9 0.3 lt.51
  35.7 15.5 %scatter_custom_fusion = s32[8192]{0:T(1024)S(1)} fusion(s32[4096]{0:T(1024)S(1)} %bitcast.64, s32[4096]{0:T(1024)S(1)} %fusion.98, s32[]{:T(128)} %constant.25.clone.1), kind=kCustom, calls=%fused_computation.188 | custom fusion | bytes 32772 | tf_op jit(solution)/shard_map/scatter | solution.py:80
  51.3 0.6 copy.221
  51.9 4.3 %all-to-all-start = ((s32[8,4,256]{2,0,1:T(8,128)}), s32[8,4,256]{2,0,1:T(8,128)S(1)}, u32[]{:S(2)}, u32[]{:S(2)}) async-start(s32[8,4,256]{2,0,1:T(8,128)} %copy.221), calls=%async_computation | async-start | bytes 65536 | tf_op jit(solution)/shard_map/all_to_all | solution.py:93
  56.3 0.4 fusion.109
  61.7 0.4 copy-done.3
  62.2 0.3 convolution_bitcast_fusion.1
  63.1 0.4 broadcast_in_dim.61
  63.4 13.8 %scatter_custom_fusion.1 = bf16[8192,128]{1,0:T(8,128)(2,1)S(1)} fusion(s32[4096]{0:T(1024)S(1)} %bitcast.65, bf16[4096,128]{1,0:T(8,128)(2,1)S(1)} %bitcast.58, bf16[]{:T(256)} %constant.49.clone.1, pred[4096]{0:T(1024)(128)(4,1)S(1)} %lt.51), kind=kCustom, calls=%fused_computation.14 | custom fusion | flops 524288 | bytes 3150848 | tf_op jit(solution)/shard_map/scatter | solution.py:75
  77.2 1.5 copy.227
  78.7 3.6 %all-to-all-start.2 = ((bf16[8,4,256,128]{3,2,0,1:T(8,128)(2,1)}), bf16[8,4,256,128]{3,2,0,1:T(8,128)(2,1)S(1)}, u32[]{:S(2)}, u32[]{:S(2)}) async-start(bf16[8,4,256,128]{3,2,0,1:T(8,128)(2,1)} %copy.227), calls=%async_computation.2 | async-start | bytes 4194304 | tf_op jit(solution)/shard_map/all_to_all | solution.py:86
  82.3 0.6 copy.222
  82.9 25.0 %all-to-all-done.2 = bf16[8,4,256,128]{3,2,0,1:T(8,128)(2,1)S(1)} async-done(((bf16[8,4,256,128]{3,2,0,1:T(8,128)(2,1)}), bf16[8,4,256,128]{3,2,0,1:T(8,128)(2,1)S(1)}, u32[]{:S(2)}, u32[]{:S(2)}) %all-to-all-start.2) | async-done | bytes 2097184 | tf_op jit(solution)/shard_map/all_to_all | solution.py:86
  107.9 6.3 %all-to-all-start.1 = ((s32[8,4,256]{2,1,0:T(4,128)}), s32[8,4,256]{2,1,0:T(4,128)S(1)}, u32[]{:S(2)}, u32[]{:S(2)}) async-start(s32[8,4,256]{2,1,0:T(4,128)} %copy.222), calls=%async_computation.1 | async-start | bytes 65536 | tf_op jit(solution)/shard_map/all_to_all | solution.py:92
  114.2 1.5 copy.228
  115.7 5.2 %all-to-all-done.1 = s32[8,4,256]{2,1,0:T(4,128)S(1)} async-done(((s32[8,4,256]{2,1,0:T(4,128)}), s32[8,4,256]{2,1,0:T(4,128)S(1)}, u32[]{:S(2)}, u32[]{:S(2)}) %all-to-all-start.1) | async-done | bytes 32800 | tf_op jit(solution)/shard_map/all_to_all | solution.py:92
  120.9 3.6 %all-to-all-start.3 = ((bf16[8,4,256,128]{3,2,1,0:T(8,128)(2,1)}), bf16[8,4,256,128]{3,2,1,0:T(8,128)(2,1)S(1)}, u32[]{:S(2)}, u32[]{:S(2)}) async-start(bf16[8,4,256,128]{3,2,1,0:T(8,128)(2,1)} %copy.228), calls=%async_computation.3 | async-start | bytes 4194304 | tf_op jit(solution)/shard_map/all_to_all | solution.py:85
  124.8 1.0 convolution_bitcast_fusion.2
  125.8 147.7 %all-reduce.2.cloned.1.call-done = f32[7,128,128]{1,2,0:T(8,128)} async-done(((f32[7,128,128]{1,2,0:T(8,128)}), f32[7,128,128]{1,2,0:T(8,128)}) %all-reduce.2.cloned.1.call-update) | async-done | bytes 458768 | tf_op jit(solution)/shard_map/psum | solution.py:35
  273.5 2.0 copy.229
  275.5 55.8 %scatter_custom_fusion.2 = f32[2049,128]{1,0:T(8,128)S(1)} fusion(s32[8192]{0:T(1024)S(1)} %bitcast.63, bf16[8192,128]{1,0:T(8,128)(2,1)S(1)} %bitcast.56, f32[]{:T(128)} %constant.21.clone.1), kind=kCustom, calls=%fused_computation.4 | custom fusion | flops 2097152 | bytes 3146244 | tf_op jit(solution)/shard_map/scatter-add | solution.py:100
  331.3 1.0 slice_bitcast_fusion
  (89 shorter events, 7.6 us)
Async XLA Ops:
  7.2 1.3 copy-start
  8.5 26.1 %copy-start.7 = (s32[128,8]{0,1:T(8,128)S(1)}, s32[128,8]{0,1:T(8,128)}, u32[]{:S(2)}) copy-start(s32[128,8]{0,1:T(8,128)} %param.10) | copy-start | bytes 12292
  34.0 22.2 %copy-start.6 = (bf16[128,28,128]{2,0,1:T(8,128)(2,1)S(1)}, bf16[128,28,128]{2,0,1:T(8,128)(2,1)}, u32[]{:S(2)}) copy-start(bf16[128,28,128]{2,0,1:T(8,128)(2,1)} %param.7) | copy-start | bytes 2752516
  34.3 22.0 %copy-start.1 = (bf16[128,8,128]{2,1,0:T(8,128)(2,1)S(1)}, bf16[128,8,128]{2,1,0:T(8,128)(2,1)}, u32[]{:S(2)}) copy-start(bf16[128,8,128]{2,1,0:T(8,128)(2,1)} %param.6) | copy-start | bytes 786436
  51.9 26.8 %all-to-all-start = ((s32[8,4,256]{2,0,1:T(8,128)}), s32[8,4,256]{2,0,1:T(8,128)S(1)}, u32[]{:S(2)}, u32[]{:S(2)}) async-start(s32[8,4,256]{2,0,1:T(8,128)} %copy.221), calls=%async_computation | async-start | bytes 65536 | tf_op jit(solution)/shard_map/all_to_all | solution.py:93
  57.3 4.2 %copy-start.5 = (bf16[7,128,128]{2,1,0:T(8,128)(2,1)S(1)}, bf16[7,128,128]{2,1,0:T(8,128)(2,1)}, u32[]{:S(2)}) copy-start(bf16[7,128,128]{2,1,0:T(8,128)(2,1)} %param.8) | copy-start | bytes 688132
  61.5 0.7 copy-start.3
  78.7 29.2 %all-to-all-start.2 = ((bf16[8,4,256,128]{3,2,0,1:T(8,128)(2,1)}), bf16[8,4,256,128]{3,2,0,1:T(8,128)(2,1)S(1)}, u32[]{:S(2)}, u32[]{:S(2)}) async-start(bf16[8,4,256,128]{3,2,0,1:T(8,128)(2,1)} %copy.227), calls=%async_computation.2 | async-start | bytes 4194304 | tf_op jit(solution)/shard_map/all_to_all | solution.py:86
  107.9 13.0 %all-to-all-start.1 = ((s32[8,4,256]{2,1,0:T(4,128)}), s32[8,4,256]{2,1,0:T(4,128)S(1)}, u32[]{:S(2)}, u32[]{:S(2)}) async-start(s32[8,4,256]{2,1,0:T(4,128)} %copy.222), calls=%async_computation.1 | async-start | bytes 65536 | tf_op jit(solution)/shard_map/all_to_all | solution.py:92
  115.7 9.1 %copy-start.2 = (bf16[128,8,128]{2,1,0:T(8,128)(2,1)S(1)}, bf16[128,8,128]{2,1,0:T(8,128)(2,1)}, u32[]{:S(2)}) copy-start(bf16[128,8,128]{2,1,0:T(8,128)(2,1)} %param.6) | copy-start | bytes 786436
  115.7 9.1 %copy-start.4 = (bf16[128,7,128]{0,2,1:T(8,128)(2,1)S(1)}, bf16[128,7,128]{0,2,1:T(8,128)(2,1)}, u32[]{:S(2)}) copy-start(bf16[128,7,128]{0,2,1:T(8,128)(2,1)} %copy-done.3) | copy-start | bytes 688132
  120.9 154.6 %all-to-all-start.3 = ((bf16[8,4,256,128]{3,2,1,0:T(8,128)(2,1)}), bf16[8,4,256,128]{3,2,1,0:T(8,128)(2,1)S(1)}, u32[]{:S(2)}, u32[]{:S(2)}) async-start(bf16[8,4,256,128]{3,2,1,0:T(8,128)(2,1)} %copy.228), calls=%async_computation.3 | async-start | bytes 4194304 | tf_op jit(solution)/shard_map/all_to_all | solution.py:85
  124.5 149.0 %all-reduce.2.cloned.1.call-start = ((), (), s32[]{:S(2)}) async-start(), calls=%async_computation.4 | async-start | bytes 917504 | tf_op jit(solution)/shard_map/psum | solution.py:35
Sparse Core Ops, SparseCore 0:
  131.2 142.2 all-reduce.1
where the time goes:
time: 340 us; the launch traced here: 339 us
  waiting for transfers between devices  178 us (52%)
  other arithmetic  71.7 us (21%)
  local copies, waits for them, and re-layouts  55.3 us (16%)
  starting transfers between devices  18 us (5%)
  between operations  14.5 us (4%)
    psum x1, waiting for transfers between devices, on_device(): weight_grad = lax.psum(local_weight, ('gx', 'gy'))  148 us
    scatter-add x1, other arithmetic, on_device(): jax.ops.segment_sum(got_values.reshape(-1, width).astype(jnp.float32), go...  55.8 us
    gather x1, local copies, waits for them, and re-layouts, on_device(): stored = row_home[field_index, bag_ids]  25.5 us
    all_to_all x1, waiting for transfers between devices, on_device(): lax.all_to_all(send_values, 'gy', split_axis=1, concat_axis=1, tiled=True)  25 us
    scatter x1, local copies, waits for them, and re-layouts, on_device(): send_target = jnp.full((owners_all * capacity,), sentinel, jnp.int32).at[...  15.5 us
    scatter x1, other arithmetic, on_device(): send_values = jnp.zeros((owners_all * capacity, width), jnp.bfloat16).at[...  13.8 us
    unnamed x55, local copies, waits for them, and re-layouts  6.81 us
  transfers between devices with their start and end apart: 5, of which 3 were waited for; matrix products, arithmetic and copies ran while one was open for 8% of the time, Pallas kernels for 0%

commit v1 on v0

--- a/solution.py
+++ b/solution.py
@@ -6,6 +6,10 @@
 FIELDS = 8
 BAG = 4
 R_DEV = 256
+
+
+def _build_ports(array_in):
+    return lax.psum(lax.psum(array_in, axis_name="gy"), axis_name="gx")
 
 
 def pair_list(fields):
@@ -32,7 +36,7 @@
     local_weight = jnp.einsum(
         "bfd,bfe->fde", pooled[:, : FIELDS - 1], upper_bf, preferred_element_type=jnp.float32
     )
-    weight_grad = lax.psum(local_weight, ("gx", "gy"))
+    weight_grad = _build_ports(local_weight)
     back_terms = jnp.einsum("bfe,fde->bfd", upper_bf, bilinear, preferred_element_type=jnp.float32)
     field_list = []
     for i in range(FIELDS):

time: 340 us -> 304 us (0.89)
  waiting for transfers between devices: 178 us -> 142 us
    psum x1 -> x2, waiting for transfers between devices: 148 us -> 112 us  [_build_ports(): return lax.psum(lax.psum(array_in, axis_name='gy'), axis_name='gx')]
  transfers between devices with their start and end apart: 5 -> 6, of which waited for: 3 -> 4; matrix products, arithmetic and copies ran while one was open for 8% -> 9% of each run, Pallas kernels for 0% -> 0%
where the time goes in v1:
time: 304 us; the launch traced here: 303 us
  waiting for transfers between devices  142 us (47%)
  other arithmetic  71.7 us (24%)
  local copies, waits for them, and re-layouts  55.3 us (18%)
  starting transfers between devices  17.9 us (6%)
  between operations  14.5 us (5%)
    psum x2, waiting for transfers between devices, _build_ports(): return lax.psum(lax.psum(array_in, axis_name='gy'), axis_name='gx')  112 us
    scatter-add x1, other arithmetic, on_device(): jax.ops.segment_sum(got_values.reshape(-1, width).astype(jnp.float32), go...  55.8 us
    gather x1, local copies, waits for them, and re-layouts, on_device(): stored = row_home[field_index, bag_ids]  25.5 us
    all_to_all x1, waiting for transfers between devices, on_device(): lax.all_to_all(send_values, 'gy', split_axis=1, concat_axis=1, tiled=True)  25 us
    scatter x1, local copies, waits for them, and re-layouts, on_device(): send_target = jnp.full((owners_all * capacity,), sentinel, jnp.int32).at[...  15.5 us
    scatter x1, other arithmetic, on_device(): send_values = jnp.zeros((owners_all * capacity, width), jnp.bfloat16).at[...  13.8 us
    unnamed x55, local copies, waits for them, and re-layouts  6.81 us
    all_to_all x1, starting transfers between devices, on_device(): lax.all_to_all(lax.all_to_all(send_target, 'gy', split_axis=1, concat_axi...  6.3 us
  transfers between devices with their start and end apart: 6, of which 4 were waited for; matrix products, arithmetic and copies ran while one was open for 9% of the time, Pallas kernels for 0%

profile of v1, /device:TPU:0, one launch (start us, length us, event | category | flops | bytes accessed | tf_op | source)
XLA Modules:
  0.0 303.1 jit_solution(15989298663088115606)
XLA Ops:
  7.2 0.8 fusion.102
  8.5 25.5 %gather_fusion = s32[4096]{0:T(1024)S(1)} fusion(s32[8,8192]{1,0:T(8,128)S(1)} %copy-done, s32[4096]{0:T(1024)S(1)} %reshape.231), kind=kCustom, calls=%fused_computation | custom fusion | bytes 65536 | tf_op jit(solution)/shard_map/gather | solution.py:56
  34.9 0.3 lt.51
  35.7 15.5 %scatter_custom_fusion = s32[8192]{0:T(1024)S(1)} fusion(s32[4096]{0:T(1024)S(1)} %bitcast.64, s32[4096]{0:T(1024)S(1)} %fusion.98, s32[]{:T(128)} %constant.25.clone.1), kind=kCustom, calls=%fused_computation.188 | custom fusion | bytes 32772 | tf_op jit(solution)/shard_map/scatter | solution.py:84
  51.3 0.6 copy.221
  51.9 4.3 %all-to-all-start = ((s32[8,4,256]{2,0,1:T(8,128)}), s32[8,4,256]{2,0,1:T(8,128)S(1)}, u32[]{:S(2)}, u32[]{:S(2)}) async-start(s32[8,4,256]{2,0,1:T(8,128)} %copy.221), calls=%async_computation | async-start | bytes 65536 | tf_op jit(solution)/shard_map/all_to_all | solution.py:97
  56.3 0.4 fusion.109
  61.7 0.4 copy-done.3
  63.1 0.4 broadcast_in_dim.61
  63.4 13.8 %scatter_custom_fusion.1 = bf16[8192,128]{1,0:T(8,128)(2,1)S(1)} fusion(s32[4096]{0:T(1024)S(1)} %bitcast.65, bf16[4096,128]{1,0:T(8,128)(2,1)S(1)} %bitcast.58, bf16[]{:T(256)} %constant.49.clone.1, pred[4096]{0:T(1024)(128)(4,1)S(1)} %lt.51), kind=kCustom, calls=%fused_computation.14 | custom fusion | flops 524288 | bytes 3150848 | tf_op jit(solution)/shard_map/scatter | solution.py:79
  77.2 1.5 copy.227
  78.7 3.6 %all-to-all-start.2 = ((bf16[8,4,256,128]{3,2,0,1:T(8,128)(2,1)}), bf16[8,4,256,128]{3,2,0,1:T(8,128)(2,1)S(1)}, u32[]{:S(2)}, u32[]{:S(2)}) async-start(bf16[8,4,256,128]{3,2,0,1:T(8,128)(2,1)} %copy.227), calls=%async_computation.2 | async-start | bytes 4194304 | tf_op jit(solution)/shard_map/all_to_all | solution.py:90
  82.3 0.6 copy.222
  82.9 25.0 %all-to-all-done.2 = bf16[8,4,256,128]{3,2,0,1:T(8,128)(2,1)S(1)} async-done(((bf16[8,4,256,128]{3,2,0,1:T(8,128)(2,1)}), bf16[8,4,256,128]{3,2,0,1:T(8,128)(2,1)S(1)}, u32[]{:S(2)}, u32[]{:S(2)}) %all-to-all-start.2) | async-done | bytes 2097184 | tf_op jit(solution)/shard_map/all_to_all | solution.py:90
  107.9 6.3 %all-to-all-start.1 = ((s32[8,4,256]{2,1,0:T(4,128)}), s32[8,4,256]{2,1,0:T(4,128)S(1)}, u32[]{:S(2)}, u32[]{:S(2)}) async-start(s32[8,4,256]{2,1,0:T(4,128)} %copy.222), calls=%async_computation.1 | async-start | bytes 65536 | tf_op jit(solution)/shard_map/all_to_all | solution.py:96
  114.2 1.5 copy.228
  115.7 5.2 %all-to-all-done.1 = s32[8,4,256]{2,1,0:T(4,128)S(1)} async-done(((s32[8,4,256]{2,1,0:T(4,128)}), s32[8,4,256]{2,1,0:T(4,128)S(1)}, u32[]{:S(2)}, u32[]{:S(2)}) %all-to-all-start.1) | async-done | bytes 32800 | tf_op jit(solution)/shard_map/all_to_all | solution.py:96
  120.9 3.6 %all-to-all-start.3 = ((bf16[8,4,256,128]{3,2,1,0:T(8,128)(2,1)}), bf16[8,4,256,128]{3,2,1,0:T(8,128)(2,1)S(1)}, u32[]{:S(2)}, u32[]{:S(2)}) async-start(bf16[8,4,256,128]{3,2,1,0:T(8,128)(2,1)} %copy.228), calls=%async_computation.3 | async-start | bytes 4194304 | tf_op jit(solution)/shard_map/all_to_all | solution.py:89
  124.6 1.0 convolution_bitcast_fusion.2
  125.6 36.1 %all-reduce.3.cloned.1.call-done = f32[7,128,128]{1,2,0:T(8,128)} async-done(((f32[7,128,128]{1,2,0:T(8,128)}), f32[7,128,128]{1,2,0:T(8,128)}) %all-reduce.3.cloned.1.call-update) | async-done | bytes 458768 | tf_op jit(solution)/shard_map/psum | solution.py:12
  161.8 75.6 %all-reduce.5.cloned.1.call-done = f32[7,128,128]{1,2,0:T(8,128)} async-done(((f32[7,128,128]{1,2,0:T(8,128)}), f32[7,128,128]{1,2,0:T(8,128)}) %all-reduce.5.cloned.1.call-update) | async-done | bytes 458768 | tf_op jit(solution)/shard_map/psum | solution.py:12
  237.4 2.0 copy.229
  239.4 55.8 %scatter_custom_fusion.2 = f32[2049,128]{1,0:T(8,128)S(1)} fusion(s32[8192]{0:T(1024)S(1)} %bitcast.63, bf16[8192,128]{1,0:T(8,128)(2,1)S(1)} %bitcast.56, f32[]{:T(128)} %constant.21.clone.1), kind=kCustom, calls=%fused_computation.4 | custom fusion | flops 2097152 | bytes 3146244 | tf_op jit(solution)/shard_map/scatter-add | solution.py:104
  295.2 1.0 slice_bitcast_fusion
  (92 shorter events, 7.8 us)
Async XLA Ops:
  7.2 1.3 copy-start
  8.5 26.1 %copy-start.7 = (s32[128,8]{0,1:T(8,128)S(1)}, s32[128,8]{0,1:T(8,128)}, u32[]{:S(2)}) copy-start(s32[128,8]{0,1:T(8,128)} %param.10) | copy-start | bytes 12292
  34.0 22.2 %copy-start.6 = (bf16[128,28,128]{2,0,1:T(8,128)(2,1)S(1)}, bf16[128,28,128]{2,0,1:T(8,128)(2,1)}, u32[]{:S(2)}) copy-start(bf16[128,28,128]{2,0,1:T(8,128)(2,1)} %param.7) | copy-start | bytes 2752516
  34.3 22.0 %copy-start.1 = (bf16[128,8,128]{2,1,0:T(8,128)(2,1)S(1)}, bf16[128,8,128]{2,1,0:T(8,128)(2,1)}, u32[]{:S(2)}) copy-start(bf16[128,8,128]{2,1,0:T(8,128)(2,1)} %param.6) | copy-start | bytes 786436
  51.9 26.8 %all-to-all-start = ((s32[8,4,256]{2,0,1:T(8,128)}), s32[8,4,256]{2,0,1:T(8,128)S(1)}, u32[]{:S(2)}, u32[]{:S(2)}) async-start(s32[8,4,256]{2,0,1:T(8,128)} %copy.221), calls=%async_computation | async-start | bytes 65536 | tf_op jit(solution)/shard_map/all_to_all | solution.py:97
  57.3 4.2 %copy-start.5 = (bf16[7,128,128]{2,1,0:T(8,128)(2,1)S(1)}, bf16[7,128,128]{2,1,0:T(8,128)(2,1)}, u32[]{:S(2)}) copy-start(bf16[7,128,128]{2,1,0:T(8,128)(2,1)} %param.8) | copy-start | bytes 688132
  61.5 0.7 copy-start.3
  78.7 29.3 %all-to-all-start.2 = ((bf16[8,4,256,128]{3,2,0,1:T(8,128)(2,1)}), bf16[8,4,256,128]{3,2,0,1:T(8,128)(2,1)S(1)}, u32[]{:S(2)}, u32[]{:S(2)}) async-start(bf16[8,4,256,128]{3,2,0,1:T(8,128)(2,1)} %copy.227), calls=%async_computation.2 | async-start | bytes 4194304 | tf_op jit(solution)/shard_map/all_to_all | solution.py:90
  107.9 13.0 %all-to-all-start.1 = ((s32[8,4,256]{2,1,0:T(4,128)}), s32[8,4,256]{2,1,0:T(4,128)S(1)}, u32[]{:S(2)}, u32[]{:S(2)}) async-start(s32[8,4,256]{2,1,0:T(4,128)} %copy.222), calls=%async_computation.1 | async-start | bytes 65536 | tf_op jit(solution)/shard_map/all_to_all | solution.py:96
  115.7 8.9 %copy-start.2 = (bf16[128,8,128]{2,1,0:T(8,128)(2,1)S(1)}, bf16[128,8,128]{2,1,0:T(8,128)(2,1)}, u32[]{:S(2)}) copy-start(bf16[128,8,128]{2,1,0:T(8,128)(2,1)} %param.6) | copy-start | bytes 786436
  115.7 8.9 %copy-start.4 = (bf16[128,7,128]{0,2,1:T(8,128)(2,1)S(1)}, bf16[128,7,128]{0,2,1:T(8,128)(2,1)}, u32[]{:S(2)}) copy-start(bf16[128,7,128]{0,2,1:T(8,128)(2,1)} %copy-done.3) | copy-start | bytes 688132
  120.9 118.5 %all-to-all-start.3 = ((bf16[8,4,256,128]{3,2,1,0:T(8,128)(2,1)}), bf16[8,4,256,128]{3,2,1,0:T(8,128)(2,1)S(1)}, u32[]{:S(2)}, u32[]{:S(2)}) async-start(bf16[8,4,256,128]{3,2,1,0:T(8,128)(2,1)} %copy.228), calls=%async_computation.3 | async-start | bytes 4194304 | tf_op jit(solution)/shard_map/all_to_all | solution.py:89
  124.5 37.2 %all-reduce.3.cloned.1.call-start = ((), (), s32[]{:S(2)}) async-start(), calls=%async_computation.4 | async-start | bytes 917504 | tf_op jit(solution)/shard_map/psum | solution.py:12
  125.6 111.9 %all-reduce.5.cloned.1.call-start = ((), (), s32[]{:S(2)}) async-start(), calls=%async_computation.5 | async-start | bytes 917504 | tf_op jit(solution)/shard_map/psum | solution.py:12
Sparse Core Ops, SparseCore 0:
  128.3 33.4 all-reduce.2
  165.2 72.2 all-reduce.4
